TPU v7x, 32 devices: a whole 2x2x4 slice. The times are simulated.
32 devices in a mesh: chan: 2 (over y), row: 8 (over z, x), col: 2 (over core).
Axes of the slice: x: 2, y: 2, z: 4, core: 2. Of those that a mesh axis runs over, the one named last changes fastest.
Arguments:
- hamiltonian_rows: float32 [16, 2, 2, 65536], P('chan', 'col', None, 'row'), parts along dimension 0, may hold values from -2 to 2, as said below
- current_block: float32 [131072, 256], P(('chan', 'row', 'col')), parts along dimension 0, may hold values from -6 to 6
- correction_block: float32 [131072, 256], P(('chan', 'row', 'col')), parts along dimension 0, may hold values from -6 to 6
- previous_block: float32 [131072, 256], P(('chan', 'row', 'col')), parts along dimension 0, may hold values from -6 to 6
- ritz_values: float32 [512], P('chan'), parts along dimension 0, may hold values from -2 to 2
- mixing_coeffs: float32 [1536, 256], P('chan'), parts along dimension 0, may hold values from -0.21875 to 0.21875
Outputs:
- next_block: float32 [64, 256], P(('chan', 'row', 'col')), parts along dimension 0
- next_direction: float32 [64, 256], P(('chan', 'row', 'col')), parts along dimension 0
- next_correction: float32 [64, 256], P(('chan', 'row', 'col')), parts along dimension 0
- ritz_matrix: float32 [512, 256], P('chan'), parts along dimension 0
- metric_matrix: float32 [512, 256], P('chan'), parts along dimension 0
There are 2 independent parts, one for each index of `chan`. A program takes and returns all parts, laid end to end along the dimension named above; each array names one. Nothing has to cross between parts.
Inputs may be any that keep to these rules, and one draw needn't show every extreme that they name: hamiltonian_rows[a, b, j, :] is row (a * 2 + b) * 4096 + j of the channel's Hamiltonian; its entry in that row's own column is the onsite energy.
All inputs are finite; a program needn't handle non-finite values.
Results may differ from a plain program's by a relative error of at most 0.00008.
Values sent between devices are 32-bit elements; how exact they have to be, the bound alone decides.
A program may use at most 128 MiB of HBM per device.

v0:
```python
import jax
import jax.numpy as jnp
from jax import lax
from jax.sharding import PartitionSpec as P


def matmul(left, right):
    return jnp.dot(left, right, preferred_element_type=jnp.float32, precision=lax.Precision.HIGHEST)


def tmatmul(left, right):
    return lax.dot_general(
        left,
        right,
        (((0,), (0,)), ((), ())),
        preferred_element_type=jnp.float32,
        precision=lax.Precision.HIGHEST,
    )


def on_device(
    hamiltonian_rows, current_block, correction_block, previous_block, ritz_values, mixing_coeffs
):
    block_width = current_block.shape[1]
    out_rows = hamiltonian_rows.shape[2]
    window_total = out_rows * lax.axis_size("row") * lax.axis_size("col")
    own_rows = jnp.concatenate([current_block, correction_block, previous_block], axis=1)
    window_rows = own_rows[:out_rows]
    mixed_rows = matmul(own_rows, mixing_coeffs)
    next_block = mixed_rows[:out_rows]
    basis_part = tmatmul(next_block, next_block)
    sent_rows = jnp.concatenate([current_block, mixed_rows], axis=1)
    gathered = lax.all_gather(sent_rows, "col", axis=0, tiled=True)
    local_tile = hamiltonian_rows.reshape(-1, hamiltonian_rows.shape[3])
    product_rows = lax.psum_scatter(
        matmul(local_tile, gathered), "row", scatter_dimension=0, tiled=True
    )
    residual = product_rows[:, :block_width] - window_rows[:, :block_width] * ritz_values[None, :]
    squares = jnp.sum(residual * residual, axis=0)
    product_part = tmatmul(next_block, product_rows[:, block_width:])
    basis_sum, product_sum, square_sum = lax.psum(
        (basis_part, product_part, squares), ("row", "col")
    )
    next_direction = matmul(window_rows[:, block_width:], mixing_coeffs[block_width:, :])
    next_correction = residual * lax.rsqrt(square_sum / window_total + 1e-06)
    return (next_block, next_direction, next_correction, product_sum, basis_sum)


def solution(mesh):
    return jax.shard_map(
        on_device,
        mesh=mesh,
        in_specs=(
            P("chan", "col", None, "row"),
            P(("chan", "row", "col"), None),
            P(("chan", "row", "col"), None),
            P(("chan", "row", "col"), None),
            P("chan"),
            P("chan", None),
        ),
        out_specs=(
            P(("chan", "row", "col"), None),
            P(("chan", "row", "col"), None),
            P(("chan", "row", "col"), None),
            P("chan", None),
            P("chan", None),
        ),
        check_vma=False,
    )
```

profile of v0, /device:TPU:0, one launch (start us, length us, event | category | flops | bytes accessed | tf_op | source)
XLA Modules:
  0.0 238.0 jit_solution(8872733745540607264)
XLA Ops:
  7.2 0.0 all-gather.2.cloned.1.call-start
  7.2 0.0 copy-start
  7.2 12.8 %fusion = f32[4096,256]{1,0:T(8,128)S(1)} fusion(f32[768,256]{1,0:T(8,128)} %param.11, f32[4096,256]{1,0:T(8,128)} %param.9, f32[4096,256]{1,0:T(8,128)} %param.8, f32[4096,256]{1,0:T(8,128)} %param.7), kind=kOutput, calls=%fused_computation | convolution fusion | flops 9669967872 | bytes 17563648 | tf_op jit(solution)/shard_map/dot_general | solution.py:8
  20.1 0.0 copy-start.1
  20.1 1.9 copy-done.1
  22.0 0.0 copy-done
  22.0 4.6 %pad_maximum_fusion = f32[4096,512]{1,0:T(8,128)} fusion(f32[4096,256]{1,0:T(8,128)S(1)} %fusion, f32[4096,256]{1,0:T(8,128)S(1)} %copy-done), kind=kLoop, calls=%fused_computation.6 | loop fusion | flops 2097152 | bytes 16777216 | tf_op jit(solution)/shard_map/concatenate | solution.py:32
  26.6 0.0 copy-start.2
  26.6 0.0 copy-start.6
  26.6 0.0 copy-start.3
  26.6 0.0 all-gather.2.cloned.1.call-update
  26.6 0.0 all-reduce.4.cloned.1.call-start
  26.6 0.8 slice.29
  27.4 0.0 copy-start.4
  27.4 0.2 copy-done.2
  27.6 0.4 reshape.15
  28.0 0.0 copy-done.6
  28.0 0.6 dynamic-slice
  29.2 1.1 fusion.13
  30.4 0.0 copy-done.3
  30.4 1.6 fusion.6
  32.0 0.0 copy-start.5
  32.0 27.6 %all-gather.2.cloned.1.call-done = f32[8192,512]{1,0:T(8,128)} async-done(((f32[4096,512]{1,0:T(8,128)}), f32[8192,512]{1,0:T(8,128)}) %all-gather.2.cloned.1.call-update) | async-done | bytes 16777232 | tf_op jit(solution)/shard_map/all_gather | solution.py:33
  59.5 11.6 %convolution_bitcast_fusion = f32[16,512]{1,0:T(8,128)S(1)} fusion(f32[8192,512]{1,0:T(8,128)} %all-gather.2.cloned.1.call-done, f32[16,8192]{1,0:T(8,128)S(1)} %reshape.15), kind=kOutput, calls=%fused_computation.7 | convolution fusion | flops 805306368 | bytes 17334272 | tf_op jit(solution)/shard_map/dot_general | solution.py:8
  71.1 37.4 %all-reduce = f32[16,512]{1,0:T(8,128)S(1)} all-reduce(f32[16,512]{1,0:T(8,128)S(1)} %convolution_bitcast_fusion), channel_id=2, replica_groups=mesh['chan'=2,'row'=8,'col'=2] {'row'}, use_global_device_ids=true, to_apply=%region_0.0.clone | all-reduce | flops 8192 | bytes 65536
  108.5 0.0 copy-done.5
  108.5 0.7 multiply_reduce_fusion
  109.2 29.5 %psum.21 = f32[256]{0:T(256)S(1)} all-reduce(f32[256]{0:T(256)S(1)} %multiply_reduce_fusion), channel_id=1, replica_groups=mesh['chan'=2,'row'=8,'col'=2] {'row','col'}, use_global_device_ids=true, to_apply=%region_2.0 | all-reduce | flops 256 | bytes 2048 | tf_op jit(solution)/shard_map/psum | solution.py:41
  138.7 0.0 copy-done.4
  138.7 1.1 fusion.9
  139.8 0.0 all-reduce.4.cloned.1.call-update
  139.9 1.3 broadcast_multiply_fusion
  141.1 86.7 %all-reduce.4.cloned.1.call-done = (f32[256,256]{1,0:T(8,128)}, f32[256,256]{1,0:T(8,128)}) async-done(((f32[256,256]{1,0:T(8,128)}, f32[256,256]{1,0:T(8,128)}), (f32[256,256]{1,0:T(8,128)}, f32[256,256]{1,0:T(8,128)})) %all-reduce.4.cloned.1.call-update) | async-done | bytes 524304 | tf_op jit(solution)/shard_map/psum | solution.py:41
  227.9 1.7 copy.13
  229.5 1.7 copy.14
  (1 shorter events, 0.0 us)
Async XLA Ops:
  7.2 52.4 %all-gather.2.cloned.1.call-start = ((), (), s32[]{:S(2)}) async-start(), calls=%async_computation | async-start | bytes 25165824 | tf_op jit(solution)/shard_map/all_gather | solution.py:33
  7.2 14.8 %copy-start = (f32[4096,256]{1,0:T(8,128)S(1)}, f32[4096,256]{1,0:T(8,128)}, u32[]{:S(2)}) copy-start(f32[4096,256]{1,0:T(8,128)} %param.7) | copy-start | bytes 12582916
  20.1 1.9 copy-start.1
  26.6 1.0 copy-start.2
  26.6 1.4 copy-start.6
  26.6 3.8 %copy-start.3 = (f32[768,256]{1,0:T(8,128)S(1)}, f32[768,256]{1,0:T(8,128)}, u32[]{:S(2)}) copy-start(f32[768,256]{1,0:T(8,128)} %param.11) | copy-start | bytes 2359300
  26.6 201.3 %all-reduce.4.cloned.1.call-start = ((), (), s32[]{:S(2)}) async-start(), calls=%async_computation.1 | async-start | bytes 1048576 | tf_op jit(solution)/shard_map/psum | solution.py:41
  27.4 111.2 %copy-start.4 = (f32[2,256]{1,0:T(2,128)}, f32[2,256]{1,0:T(2,128)S(1)}, u32[]{:S(2)}) copy-start(f32[2,256]{1,0:T(2,128)S(1)} %slice.29) | copy-start | bytes 6148
  32.0 76.5 %copy-start.5 = (f32[256]{0:T(256)S(1)}, f32[256]{0:T(256)}, u32[]{:S(2)}) copy-start(f32[256]{0:T(256)} %param.10) | copy-start | bytes 3076
Sparse Core Ops, SparseCore 0:
  26.7 32.7 all-gather.1
  140.0 87.8 all-reduce.3
where the time goes:
time: 239 us; the launch traced here: 238 us
  waiting for transfers between devices  114 us (48%)
  blocking collectives  66.8 us (28%)
  matrix products  28.3 us (12%)
  between operations  14.8 us (6%)
  local copies, waits for them, and re-layouts  7.2 us (3%)
  other arithmetic  6.56 us (3%)
    psum x1, waiting for transfers between devices, on_device(): lax.psum((basis_part, product_part, squares), ('row', 'col'))  86.7 us
    unnamed x1, blocking collectives  37.4 us
    psum x1, blocking collectives, on_device(): lax.psum((basis_part, product_part, squares), ('row', 'col'))  29.5 us
    all_gather x1, waiting for transfers between devices, on_device(): gathered = lax.all_gather(sent_rows, 'col', axis=0, tiled=True)  27.6 us
    dot_general x3, matrix products, matmul(): jnp.dot(left, right, preferred_element_type=jnp.float32, precision=lax.Pr...  26 us
    unnamed x17, local copies, waits for them, and re-layouts  6.06 us
  transfers between devices with their start and end apart: 2, of which 2 were waited for; matrix products, arithmetic and copies ran while one was open for 2% of the time, Pallas kernels for 0%

commit v1 on v0

v1 whole, which is shorter than its diff:
```python
import functools

import jax
import jax.numpy as jnp
from jax import lax
from jax.experimental import pallas as pl
from jax.experimental.pallas import tpu as pltpu
from jax.sharding import PartitionSpec as P

MESH = pl.DeviceIdType.MESH
F32 = jnp.float32
BF16 = jnp.bfloat16


def split(x):
    hi = x.astype(BF16)
    return hi, (x - hi.astype(F32)).astype(BF16)


def stack(x):
    return jnp.concatenate(split(x), axis=0)


def dot(a, b):
    return jnp.dot(a, b, preferred_element_type=F32)


def fold(x):
    half = x.shape[0] // 2
    return x[:half] + x[half:]


def tdot(at, b):
    return lax.dot_general(at, b, (((0,), (0,)), ((), ())), preferred_element_type=F32)


def kernel(
    n_row, n_col, chunks,
    h_ref, x_ref, w_ref, p_ref, ritz_ref, mix_ref,
    nb_out, nd_out, nc_out, rm_out, mm_out,
    hbuf, hsend, hf, hst, base, bhi, blo, top, mixf, mhi, mlo, ritz_v, acc,
    nb_all, rs_send, rs_recv, ag_all, nb_f, zm_f,
    base_sem, top_sem, mix_sem, ritz_sem, own_sem, stage_sem,
    h_sems, nb_sems, rs_sems, ag_sems,
):
    n = n_row * n_col
    row, col = lax.axis_index("row"), lax.axis_index("col")
    me = row * n_col + col
    blocks = (x_ref, w_ref, p_ref)
    out_rows = h_ref.shape[2]
    local, width = x_ref.shape
    step = local // chunks
    win = n * out_rows
    unroll = n <= 32

    def peers(body):
        def one(i, carry):
            p = lax.rem(me + i, n)
            body(p, {"row": p // n_col, "col": lax.rem(p, n_col)})
            return carry
        lax.fori_loop(1, n, one, 0, unroll=unroll)

    def cols(c):
        return pl.ds(pl.multiple_of(c * local, 128), local)

    def partner(i):
        return lax.rem(col + i, n_col)

    def stage(i):
        return pltpu.make_async_copy(h_ref.at[:, 0, :, cols(partner(i))], hsend.at[i - 1], stage_sem.at[i - 1])

    own = pltpu.make_async_copy(h_ref.at[:, 0, :, cols(col)], hbuf.at[col], own_sem)
    mix_copy = pltpu.make_async_copy(mix_ref, mixf, mix_sem)
    ritz_copy = pltpu.make_async_copy(ritz_ref, ritz_v, ritz_sem)

    def top_copy(b):
        return pltpu.make_async_copy(blocks[b].at[pl.ds(0, 8), :], top.at[b], top_sem.at[b])

    def base_copy(b, k):
        rows = pl.ds(pl.multiple_of(k * step, 8), step)
        return pltpu.make_async_copy(blocks[b].at[rows, :], base.at[b, rows, :], base_sem.at[b, k])

    for i in range(1, n_col):
        stage(i).start()
    for b in range(3):
        top_copy(b).start()
    mix_copy.start()
    own.start()
    ritz_copy.start()

    def start_base(k, carry):
        for b in range(3):
            base_copy(b, k).start()
        return carry
    lax.fori_loop(0, chunks, start_base, 0)

    barrier = pltpu.get_barrier_semaphore()
    peers(lambda p, dev: pl.semaphore_signal(barrier, inc=1, device_id=dev, device_id_type=MESH))

    for b in range(3):
        top_copy(b).wait()
    mix_copy.wait()
    hi, lo = split(mixf[...])
    mhi[...] = hi
    mlo[...] = lo
    lhs = [stack(top[b]) for b in range(3)]

    def part(b):
        rows = pl.ds(b * width, width)
        return fold(dot(lhs[b], mhi[rows, :]) + dot(lhs[b], mlo[rows, :]))
    nd = part(1) + part(2)
    nb = part(0) + nd
    nb_out[...] = nb[:out_rows]
    nd_out[...] = nd[:out_rows]
    nb_all[me] = nb[:out_rows]

    def cast(k, carry):
        rows = pl.ds(pl.multiple_of(k * step, 16), step)
        for b in range(3):
            base_copy(b, k).wait()
            hi, lo = split(base[b, rows, :])
            bhi[rows, pl.ds(b * width, width)] = hi
            blo[rows, pl.ds(b * width, width)] = lo
        return carry
    early = chunks // 2
    lax.fori_loop(0, early, cast, 0)

    for i in range(1, n_col):
        stage(i).wait()
    pl.semaphore_wait(barrier, n - 1)

    def h_copy(i):
        return pltpu.make_async_remote_copy(
            src_ref=hsend.at[i - 1], dst_ref=hbuf.at[col],
            send_sem=h_sems.at[0, i - 1], recv_sem=h_sems.at[1, i - 1],
            device_id={"row": row, "col": partner(i)}, device_id_type=MESH)
    for i in range(1, n_col):
        h_copy(i).start()

    def spread(src, dst, sems):
        def one(p, dev):
            pltpu.make_async_remote_copy(
                src_ref=src(p), dst_ref=dst.at[me], send_sem=sems.at[0], recv_sem=sems.at[1],
                device_id=dev, device_id_type=MESH).start()
        peers(one)

    def gather_wait(buf, sems, which):
        view = buf.at[pl.ds(0, n - 1)]
        pltpu.make_async_copy(view, view, sems.at[which]).wait()

    spread(lambda p: nb_all.at[me], nb_all, nb_sems)
    lax.fori_loop(early, chunks, cast, 0)

    own.wait()
    for i in range(1, n_col):
        h_copy(i).wait()
    for c in range(n_col):
        for a in range(n_row):
            at = (c * n_row + a) * out_rows
            hf[at:at + out_rows, :] = hbuf[c, a]
    hi, lo = split(hf[...])
    hst[:win, :] = hi
    hst[win:, :] = lo

    acc[...] = jnp.zeros_like(acc)

    def multiply(k, carry):
        rows = pl.ds(pl.multiple_of(k * step, 128), step)
        left = hst[:, rows]
        acc[...] += dot(left, bhi[rows, :]) + dot(left, blo[rows, :])
        return carry
    lax.fori_loop(0, chunks, multiply, 0)

    product = fold(acc[...])
    lhs2 = stack(product)
    mixed = fold(dot(lhs2, mhi[...]) + dot(lhs2, mlo[...]))
    for a in range(n_row):
        for c in range(n_col):
            at = (c * n_row + a) * out_rows
            rs_send[a * n_col + c, :, :width] = product[at:at + out_rows, :width]
            rs_send[a * n_col + c, :, width:] = mixed[at:at + out_rows]
    spread(lambda p: rs_send.at[p], rs_recv, rs_sems)
    rs_recv[me] = rs_send[me]

    gather_wait(nb_all, nb_sems, 1)
    for q in range(n):
        nb_f[q * out_rows:(q + 1) * out_rows, :] = nb_all[q]
    hi, lo = split(nb_f[...])
    left = jnp.concatenate([hi, hi, lo, lo], axis=0)
    mm_out[...] = tdot(left, jnp.concatenate([hi, lo, hi, lo], axis=0))
    ritz_copy.wait()

    gather_wait(rs_recv, rs_sems, 1)
    total = jnp.sum(rs_recv[...], axis=0)
    residual = total[:, :width] - top[0, :out_rows, :] * ritz_v[...]
    ag_all[me, :out_rows, :] = total[:, width:]
    ag_all[me, out_rows:out_rows + 1, :] = jnp.sum(residual * residual, axis=0, keepdims=True)
    spread(lambda p: ag_all.at[me], ag_all, ag_sems)

    gather_wait(ag_all, ag_sems, 1)
    squares = jnp.sum(ag_all[:, out_rows:out_rows + 1, :], axis=0)
    nc_out[...] = residual * lax.rsqrt(squares / win + 1e-6)
    for q in range(n):
        zm_f[q * out_rows:(q + 1) * out_rows, :] = ag_all[q, :out_rows, :]
    hi, lo = split(zm_f[...])
    rm_out[...] = tdot(left, jnp.concatenate([hi, lo, hi, lo], axis=0))
    gather_wait(nb_all, nb_sems, 0)
    gather_wait(rs_send, rs_sems, 0)
    gather_wait(ag_all, ag_sems, 0)


def solution(mesh):
    n_row, n_col = mesh.shape["row"], mesh.shape["col"]
    n = n_row * n_col

    def on_device(h, x, w, p, ritz, mix):
        local, width = x.shape
        out_rows = h.shape[2]
        win = n * out_rows
        chunks = max(local // 512, 2)
        vm = pltpu.VMEM
        dma = pltpu.SemaphoreType.DMA
        any_spec = pl.BlockSpec(memory_space=pl.ANY)
        vmem_spec = pl.BlockSpec(memory_space=pltpu.VMEM)
        return pl.pallas_call(
            functools.partial(kernel, n_row, n_col, chunks),
            out_shape=[jax.ShapeDtypeStruct((out_rows, width), F32)] * 3
            + [jax.ShapeDtypeStruct((width, width), F32)] * 2,
            in_specs=[any_spec] * 6,
            out_specs=[vmem_spec] * 5,
            scratch_shapes=[
                vm((n_col, n_row, out_rows, local), F32),
                vm((n_col - 1, n_row, out_rows, local), F32),
                vm((win, local), F32),
                vm((2 * win, local), BF16),
                vm((3, local, width), F32),
                vm((local, 3 * width), BF16),
                vm((local, 3 * width), BF16),
                vm((3, 8, width), F32),
                vm((3 * width, width), F32),
                vm((3 * width, width), BF16),
                vm((3 * width, width), BF16),
                vm((1, width), F32),
                vm((2 * win, 3 * width), F32),
                vm((n, out_rows, width), F32),
                vm((n, out_rows, 2 * width), F32),
                vm((n, out_rows, 2 * width), F32),
                vm((n, 2 * out_rows, width), F32),
                vm((win, width), F32),
                vm((win, width), F32),
                dma((3, chunks)), dma((3,)), dma, dma, dma, dma((n_col - 1,)),
                dma((2, n_col - 1)), dma((2,)), dma((2,)), dma((2,)),
            ],
            compiler_params=pltpu.CompilerParams(
                collective_id=0, has_side_effects=True, vmem_limit_bytes=60 * 1024 * 1024
            ),
        )(h, x, w, p, ritz.reshape(1, width), mix)

    blocks = P(("chan", "row", "col"), None)
    return jax.shard_map(
        on_device,
        mesh=mesh,
        in_specs=(P("chan", "col", None, "row"), blocks, blocks, blocks, P("chan"), P("chan", None)),
        out_specs=(blocks, blocks, blocks, P("chan", None), P("chan", None)),
        check_vma=False,
    )
```

time: 239 us -> 29 us (0.12)
  waiting for transfers between devices: 114 us -> 0 us
  blocking collectives: 66.8 us -> 0 us
  matrix products: 28.3 us -> 0 us
  Pallas kernels: 0 us -> 21 us
  between operations: 14.8 us -> 0.64 us
  other arithmetic: 6.56 us -> 0 us
    psum x1 -> x0, waiting for transfers between devices: 86.7 us -> none  [on_device(): lax.psum((basis_part, product_part, squares), ('row', 'col'))]
    unnamed x1 -> x0, blocking collectives: 37.4 us -> none
    psum x1 -> x0, blocking collectives: 29.5 us -> none  [on_device(): lax.psum((basis_part, product_part, squares), ('row', 'col'))]
    dot_general x5 -> x0, matrix products: 28.3 us -> none  [the longest x3 26 us: matmul(): jnp.dot(left, right, preferred_element_type=jnp.float32, precision=lax.Pr...]
    all_gather x1 -> x0, waiting for transfers between devices: 27.6 us -> none  [on_device(): gathered = lax.all_gather(sent_rows, 'col', axis=0, tiled=True)]
    pallas_call x0 -> x1, Pallas kernels: none -> 21 us  [on_device(): pl.pallas_call(functools.partial(kernel, n_row, n_col, chunks), out_shape...]
    concatenate x1 -> x0, other arithmetic: 4.55 us -> none  [on_device(): sent_rows = jnp.concatenate([current_block, mixed_rows], axis=1)]
    unnamed x17 -> x5, local copies, waits for them, and re-layouts: 6.06 us -> 7.08 us
  transfers between devices with their start and end apart: 2 -> 0, of which waited for: 2 -> 0; matrix products, arithmetic and copies ran while one was open for 2% -> 0% of each run, Pallas kernels for 0% -> 0%
where the time goes in v1:
time: 29 us; the launch traced here: 28.7 us
  Pallas kernels  21 us (72%)
  local copies, waits for them, and re-layouts  7.08 us (24%)
  between operations  0.64 us (2%)
    pallas_call x1, Pallas kernels, on_device(): pl.pallas_call(functools.partial(kernel, n_row, n_col, chunks), out_shape...  21 us
    unnamed x5, local copies, waits for them, and re-layouts  7.08 us

profile of v1, /device:TPU:0, one launch (start us, length us, event | category | flops | bytes accessed | tf_op | source)
XLA Modules:
  0.0 28.7 jit_solution(5951877639268597114)
XLA Ops:
  0.6 21.0 %shard_map.101 = (f32[2,256]{1,0:T(2,128)}, f32[2,256]{1,0:T(2,128)}, f32[2,256]{1,0:T(2,128)}, f32[256,256]{1,0:T(8,128)}, f32[256,256]{1,0:T(8,128)}) custom-call(f32[8,1,2,8192]{3,2,1,0:T(2,128)} %h_ref.1, f32[4096,256]{1,0:T(8,128)} %x_ref.1, f32[4096,256]{1,0:T(8,128)} %w_ref.1, f32[4096,256]{1,0:T(8,128)} %p_ref.1, f32[1,256]{1,0:T(1,128)} %bitcast.1, ...), custom_call_target="tpu_custom_call" | custom-call | tf_op jit(solution)/shard_map/pallas_call | solution.py:225
  21.6 1.3 %copy.16 = f32[2,256]{1,0:T(2,128)} copy(f32[2,256]{1,0:T(2,128)} %get-tuple-element.10) | data formatting | bytes 4096
  22.9 1.2 %copy.17 = f32[2,256]{1,0:T(2,128)} copy(f32[2,256]{1,0:T(2,128)} %get-tuple-element.11) | data formatting | bytes 4096
  24.1 1.2 %copy.18 = f32[2,256]{1,0:T(2,128)} copy(f32[2,256]{1,0:T(2,128)} %get-tuple-element.12) | data formatting | bytes 4096
  25.4 1.7 %copy.19 = f32[256,256]{1,0:T(8,128)} copy(f32[256,256]{1,0:T(8,128)} %get-tuple-element.13) | data formatting | bytes 524288
  27.1 1.7 %copy.20 = f32[256,256]{1,0:T(8,128)} copy(f32[256,256]{1,0:T(8,128)} %get-tuple-element.14) | data formatting | bytes 524288

commit v2 on v1

--- a/solution.py
+++ b/solution.py
@@ -37,9 +37,9 @@
 def kernel(
     n_row, n_col, chunks,
     h_ref, x_ref, w_ref, p_ref, ritz_ref, mix_ref,
-    nb_out, nd_out, nc_out, rm_out, mm_out,
+    small_out, rows_out,
     hbuf, hsend, hf, hst, base, bhi, blo, top, mixf, mhi, mlo, ritz_v, acc,
-    nb_all, rs_send, rs_recv, ag_all, nb_f, zm_f,
+    nb_all, rs_send, rs_recv, ag_all,
     base_sem, top_sem, mix_sem, ritz_sem, own_sem, stage_sem,
     h_sems, nb_sems, rs_sems, ag_sems,
 ):
@@ -110,8 +110,8 @@
         return fold(dot(lhs[b], mhi[rows, :]) + dot(lhs[b], mlo[rows, :]))
     nd = part(1) + part(2)
     nb = part(0) + nd
-    nb_out[...] = nb[:out_rows]
-    nd_out[...] = nd[:out_rows]
+    small_out[0] = nb[:out_rows]
+    small_out[1] = nd[:out_rows]
     nb_all[me] = nb[:out_rows]
 
     def cast(k, carry):
@@ -184,10 +184,7 @@
 
     gather_wait(nb_all, nb_sems, 1)
     for q in range(n):
-        nb_f[q * out_rows:(q + 1) * out_rows, :] = nb_all[q]
-    hi, lo = split(nb_f[...])
-    left = jnp.concatenate([hi, hi, lo, lo], axis=0)
-    mm_out[...] = tdot(left, jnp.concatenate([hi, lo, hi, lo], axis=0))
+        rows_out[0, q * out_rows:(q + 1) * out_rows, :] = nb_all[q]
     ritz_copy.wait()
 
     gather_wait(rs_recv, rs_sems, 1)
@@ -199,14 +196,23 @@
 
     gather_wait(ag_all, ag_sems, 1)
     squares = jnp.sum(ag_all[:, out_rows:out_rows + 1, :], axis=0)
-    nc_out[...] = residual * lax.rsqrt(squares / win + 1e-6)
+    small_out[2] = residual * lax.rsqrt(squares / win + 1e-6)
     for q in range(n):
-        zm_f[q * out_rows:(q + 1) * out_rows, :] = ag_all[q, :out_rows, :]
-    hi, lo = split(zm_f[...])
-    rm_out[...] = tdot(left, jnp.concatenate([hi, lo, hi, lo], axis=0))
+        rows_out[1, q * out_rows:(q + 1) * out_rows, :] = ag_all[q, :out_rows, :]
     gather_wait(nb_all, nb_sems, 0)
     gather_wait(rs_send, rs_sems, 0)
     gather_wait(ag_all, ag_sems, 0)
+
+
+def finish(small, rows, nb_out, nd_out, nc_out, rm_out, mm_out):
+    nb_out[...] = small[0]
+    nd_out[...] = small[1]
+    nc_out[...] = small[2]
+    hi, lo = split(rows[0])
+    left = jnp.concatenate([hi, hi, lo, lo], axis=0)
+    mm_out[...] = tdot(left, jnp.concatenate([hi, lo, hi, lo], axis=0))
+    hi, lo = split(rows[1])
+    rm_out[...] = tdot(left, jnp.concatenate([hi, lo, hi, lo], axis=0))
 
 
 def solution(mesh):
@@ -222,12 +228,11 @@
         dma = pltpu.SemaphoreType.DMA
         any_spec = pl.BlockSpec(memory_space=pl.ANY)
         vmem_spec = pl.BlockSpec(memory_space=pltpu.VMEM)
-        return pl.pallas_call(
+        small, rows = pl.pallas_call(
             functools.partial(kernel, n_row, n_col, chunks),
-            out_shape=[jax.ShapeDtypeStruct((out_rows, width), F32)] * 3
-            + [jax.ShapeDtypeStruct((width, width), F32)] * 2,
+            out_shape=[vm((3, out_rows, width), F32), vm((2, win, width), F32)],
             in_specs=[any_spec] * 6,
-            out_specs=[vmem_spec] * 5,
+            out_specs=[vmem_spec] * 2,
             scratch_shapes=[
                 vm((n_col, n_row, out_rows, local), F32),
                 vm((n_col - 1, n_row, out_rows, local), F32),
@@ -246,8 +251,6 @@
                 vm((n, out_rows, 2 * width), F32),
                 vm((n, out_rows, 2 * width), F32),
                 vm((n, 2 * out_rows, width), F32),
-                vm((win, width), F32),
-                vm((win, width), F32),
                 dma((3, chunks)), dma((3,)), dma, dma, dma, dma((n_col - 1,)),
                 dma((2, n_col - 1)), dma((2,)), dma((2,)), dma((2,)),
             ],
@@ -255,6 +258,14 @@
                 collective_id=0, has_side_effects=True, vmem_limit_bytes=60 * 1024 * 1024
             ),
         )(h, x, w, p, ritz.reshape(1, width), mix)
+        return pl.pallas_call(
+            finish,
+            out_shape=[jax.ShapeDtypeStruct((out_rows, width), F32)] * 3
+            + [jax.ShapeDtypeStruct((width, width), F32)] * 2,
+            in_specs=[vmem_spec] * 2,
+            out_specs=[vmem_spec] * 5,
+            compiler_params=pltpu.CompilerParams(vmem_limit_bytes=16 * 1024 * 1024),
+        )(small, rows)
 
     blocks = P(("chan", "row", "col"), None)
     return jax.shard_map(

time: 29 us -> 21.9 us (0.76)
  local copies, waits for them, and re-layouts: 7.08 us -> 0 us
    unnamed x5 -> x0, local copies, waits for them, and re-layouts: 7.08 us -> none
    pallas_call x0 -> x1, Pallas kernels: none -> 1.04 us  [on_device(): pl.pallas_call(finish, out_shape=[jax.ShapeDtypeStruct((out_rows, width),...]
    pallas_call x1, Pallas kernels: 21 us -> 20 us  [on_device(): pl.pallas_call(functools.partial(kernel, n_row, n_col, chunks), out_shape...]
where the time goes in v2:
time: 21.9 us; the launch traced here: 21.7 us
  Pallas kernels  21 us (96%)
  between operations  0.64 us (3%)
    pallas_call x1, Pallas kernels, on_device(): pl.pallas_call(functools.partial(kernel, n_row, n_col, chunks), out_shape...  20 us
    pallas_call x1, Pallas kernels, on_device(): pl.pallas_call(finish, out_shape=[jax.ShapeDtypeStruct((out_rows, width),...  1.04 us

profile of v2, /device:TPU:0, one launch (start us, length us, event | category | flops | bytes accessed | tf_op | source)
XLA Modules:
  0.0 21.7 jit_solution(13004273210969330781)
XLA Ops:
  0.6 20.0 %shard_map.101 = (f32[3,2,256]{2,1,0:T(2,128)S(1)}, f32[2,32,256]{2,1,0:T(8,128)S(1)}) custom-call(f32[8,1,2,8192]{3,2,1,0:T(2,128)} %h_ref.1, f32[4096,256]{1,0:T(8,128)} %x_ref.1, f32[4096,256]{1,0:T(8,128)} %w_ref.1, f32[4096,256]{1,0:T(8,128)} %p_ref.1, f32[1,256]{1,0:T(1,128)} %bitcast.1, f32[768,256]{1,0:T(8,128)} %mix_ref.1), custom_call_target="tpu_custom_call" | custom-call | tf_op jit(solution)/shard_map/pallas_call | solution.py:231
  20.6 1.0 %shard_map.102 = (f32[2,256]{1,0:T(2,128)}, f32[2,256]{1,0:T(2,128)}, f32[2,256]{1,0:T(2,128)}, f32[256,256]{1,0:T(8,128)}, f32[256,256]{1,0:T(8,128)}) custom-call(f32[3,2,256]{2,1,0:T(2,128)S(1)} %get-tuple-element.7.small, f32[2,32,256]{2,1,0:T(8,128)S(1)} %get-tuple-element.8.rows), custom_call_target="tpu_custom_call" | custom-call | tf_op jit(solution)/shard_map/pallas_call | solution.py:261

commit v3 on v2

--- a/solution.py
+++ b/solution.py
@@ -39,9 +39,9 @@
     h_ref, x_ref, w_ref, p_ref, ritz_ref, mix_ref,
     small_out, rows_out,
     hbuf, hsend, hf, hst, base, bhi, blo, top, mixf, mhi, mlo, ritz_v, acc,
-    nb_all, rs_send, rs_recv, ag_all,
+    nb_all, xs_send, xs_recv, rs_send, rs_recv, sq_all, ag_all,
     base_sem, top_sem, mix_sem, ritz_sem, own_sem, stage_sem,
-    h_sems, nb_sems, rs_sems, ag_sems,
+    h_sems, nb_sems, xs_sems, rs_sems, sq_sems, ag_sems,
 ):
     n = n_row * n_col
     row, col = lax.axis_index("row"), lax.axis_index("col")
@@ -164,43 +164,54 @@
 
     acc[...] = jnp.zeros_like(acc)
 
-    def multiply(k, carry):
-        rows = pl.ds(pl.multiple_of(k * step, 128), step)
-        left = hst[:, rows]
-        acc[...] += dot(left, bhi[rows, :]) + dot(left, blo[rows, :])
-        return carry
-    lax.fori_loop(0, chunks, multiply, 0)
-
-    product = fold(acc[...])
+    def multiply(span):
+        def one(k, carry):
+            rows = pl.ds(pl.multiple_of(k * step, 128), step)
+            left = hst[:, rows]
+            acc[:, span] += dot(left, bhi[rows, span]) + dot(left, blo[rows, span])
+            return carry
+        lax.fori_loop(0, chunks, one, 0)
+        return fold(acc[:, span])
+
+    def scatter(value, send, recv, sems):
+        for a in range(n_row):
+            for c in range(n_col):
+                at = (c * n_row + a) * out_rows
+                send[a * n_col + c] = value[at:at + out_rows]
+        spread(lambda p: send.at[p], recv, sems)
+        recv[me] = send[me]
+
+    product = multiply(slice(0, width))
+    scatter(product, xs_send, xs_recv, xs_sems)
+    product = jnp.concatenate([product, multiply(slice(width, 3 * width))], axis=1)
     lhs2 = stack(product)
     mixed = fold(dot(lhs2, mhi[...]) + dot(lhs2, mlo[...]))
-    for a in range(n_row):
-        for c in range(n_col):
-            at = (c * n_row + a) * out_rows
-            rs_send[a * n_col + c, :, :width] = product[at:at + out_rows, :width]
-            rs_send[a * n_col + c, :, width:] = mixed[at:at + out_rows]
-    spread(lambda p: rs_send.at[p], rs_recv, rs_sems)
-    rs_recv[me] = rs_send[me]
+    scatter(mixed, rs_send, rs_recv, rs_sems)
+
+    ritz_copy.wait()
+    gather_wait(xs_recv, xs_sems, 1)
+    residual = jnp.sum(xs_recv[...], axis=0) - top[0, :out_rows, :] * ritz_v[...]
+    sq_all[me] = jnp.sum(residual * residual, axis=0, keepdims=True)
+    spread(lambda p: sq_all.at[me], sq_all, sq_sems)
 
     gather_wait(nb_all, nb_sems, 1)
     for q in range(n):
         rows_out[0, q * out_rows:(q + 1) * out_rows, :] = nb_all[q]
-    ritz_copy.wait()
 
     gather_wait(rs_recv, rs_sems, 1)
-    total = jnp.sum(rs_recv[...], axis=0)
-    residual = total[:, :width] - top[0, :out_rows, :] * ritz_v[...]
-    ag_all[me, :out_rows, :] = total[:, width:]
-    ag_all[me, out_rows:out_rows + 1, :] = jnp.sum(residual * residual, axis=0, keepdims=True)
+    ag_all[me] = jnp.sum(rs_recv[...], axis=0)
     spread(lambda p: ag_all.at[me], ag_all, ag_sems)
 
+    gather_wait(sq_all, sq_sems, 1)
+    squares = jnp.sum(sq_all[...], axis=0)
+    small_out[2] = residual * lax.rsqrt(squares / win + 1e-6)
     gather_wait(ag_all, ag_sems, 1)
-    squares = jnp.sum(ag_all[:, out_rows:out_rows + 1, :], axis=0)
-    small_out[2] = residual * lax.rsqrt(squares / win + 1e-6)
     for q in range(n):
-        rows_out[1, q * out_rows:(q + 1) * out_rows, :] = ag_all[q, :out_rows, :]
+        rows_out[1, q * out_rows:(q + 1) * out_rows, :] = ag_all[q]
     gather_wait(nb_all, nb_sems, 0)
+    gather_wait(xs_send, xs_sems, 0)
     gather_wait(rs_send, rs_sems, 0)
+    gather_wait(sq_all, sq_sems, 0)
     gather_wait(ag_all, ag_sems, 0)
 
 
@@ -248,11 +259,14 @@
                 vm((1, width), F32),
                 vm((2 * win, 3 * width), F32),
                 vm((n, out_rows, width), F32),
-                vm((n, out_rows, 2 * width), F32),
-                vm((n, out_rows, 2 * width), F32),
-                vm((n, 2 * out_rows, width), F32),
+                vm((n, out_rows, width), F32),
+                vm((n, out_rows, width), F32),
+                vm((n, out_rows, width), F32),
+                vm((n, out_rows, width), F32),
+                vm((n, 1, width), F32),
+                vm((n, out_rows, width), F32),
                 dma((3, chunks)), dma((3,)), dma, dma, dma, dma((n_col - 1,)),
-                dma((2, n_col - 1)), dma((2,)), dma((2,)), dma((2,)),
+                dma((2, n_col - 1)), dma((2,)), dma((2,)), dma((2,)), dma((2,)), dma((2,)),
             ],
             compiler_params=pltpu.CompilerParams(
                 collective_id=0, has_side_effects=True, vmem_limit_bytes=60 * 1024 * 1024

time: 21.9 us -> 22.5 us (1.027)
  Pallas kernels: 21 us -> 21.6 us
    pallas_call x1, Pallas kernels: 20 us -> 20.6 us  [on_device(): pl.pallas_call(functools.partial(kernel, n_row, n_col, chunks), out_shape...]
where the time goes in v3:
time: 22.5 us; the launch traced here: 22.3 us
  Pallas kernels  21.6 us (96%)
  between operations  0.64 us (3%)
    pallas_call x1, Pallas kernels, on_device(): pl.pallas_call(functools.partial(kernel, n_row, n_col, chunks), out_shape...  20.6 us
    pallas_call x1, Pallas kernels, on_device(): pl.pallas_call(finish, out_shape=[jax.ShapeDtypeStruct((out_rows, width),...  1.04 us

profile of v3, /device:TPU:0, one launch (start us, length us, event | category | flops | bytes accessed | tf_op | source)
XLA Modules:
  0.0 22.3 jit_solution(9431461769646333479)
XLA Ops:
  0.6 20.6 %shard_map.101 = (f32[3,2,256]{2,1,0:T(2,128)S(1)}, f32[2,32,256]{2,1,0:T(8,128)S(1)}) custom-call(f32[8,1,2,8192]{3,2,1,0:T(2,128)} %h_ref.1, f32[4096,256]{1,0:T(8,128)} %x_ref.1, f32[4096,256]{1,0:T(8,128)} %w_ref.1, f32[4096,256]{1,0:T(8,128)} %p_ref.1, f32[1,256]{1,0:T(1,128)} %bitcast.1, f32[768,256]{1,0:T(8,128)} %mix_ref.1), custom_call_target="tpu_custom_call" | custom-call | tf_op jit(solution)/shard_map/pallas_call | solution.py:242
  21.2 1.0 %shard_map.102 = (f32[2,256]{1,0:T(2,128)}, f32[2,256]{1,0:T(2,128)}, f32[2,256]{1,0:T(2,128)}, f32[256,256]{1,0:T(8,128)}, f32[256,256]{1,0:T(8,128)}) custom-call(f32[3,2,256]{2,1,0:T(2,128)S(1)} %get-tuple-element.7.small, f32[2,32,256]{2,1,0:T(8,128)S(1)} %get-tuple-element.8.rows), custom_call_target="tpu_custom_call" | custom-call | tf_op jit(solution)/shard_map/pallas_call | solution.py:275
